TPU v7x, 32 devices: a whole 2x2x4 slice. The times are simulated.
32 devices in a mesh: node: 16 (over z, x, core), head: 2 (over y).
Axes of the slice: x: 2, y: 2, z: 4, core: 2. Of those that a mesh axis runs over, the one named last changes fastest.
Arguments:
- features: bfloat16 [32768, 100], P('node'), may hold values from -6 to 6
- proj_weight: bfloat16 [100, 512], P(None, 'head'), may hold values from -0.625 to 0.625
- score_src: float32 [8, 64], P('head'), may hold values from -150 to 150
- score_dst: float32 [8, 64], P('head'), may hold values from -0.75 to 0.75
- request_rows: int32 [16, 16, 512], P('node'), may hold values from 0 to 2047
- slot_index: int32 [8192, 16], P('node'), may hold values from 0 to 8191
- slot_count: int32 [8192], P('node'), may hold values from 1 to 16
- out_weight: bfloat16 [512, 512], replicated, may hold values from -0.25 to 0.25
Outputs:
- layer_out: bfloat16 [8192, 512], P(('node', 'head'))
All inputs are finite; a program needn't handle non-finite values.
Results may differ from a plain program's by a relative error of at most 0.012.
The roundings to bfloat16 on the way count: a program that leaves them out, or rounds other values in their place, can miss the bound.
Values may be sent and summed in bfloat16 or wider, within the bound.
No kernel may reach another device: no remote copies, remote signals or barrier semaphores. Data moves between devices by JAX's collectives and lax.ppermute only.
A program may use at most 64 MiB of HBM per device.

v0:
```python
import functools
import math

import jax
import jax.numpy as jnp
from jax import lax
from jax.experimental import pallas as pl
from jax.experimental.pallas import tpu as pltpu
from jax.sharding import PartitionSpec as P


LANES = 128
DEPTH = 4
GROUP = 16


def spare_split(capacity, feat):
    tucked = capacity * 3 // 16
    piece = -(-feat // 4)
    if tucked % 8 or (capacity - tucked) % 16 or feat + piece > LANES:
        return capacity, 0, piece
    return capacity - tucked, tucked, piece


def here(values):
    return pltpu.with_memory_space_constraint(values, pltpu.VMEM)


def copy_rows(index, table, out, count, start=0):
    for place in range(count):
        out[place : place + 1, :] = table[pl.ds(index[start + place], 1), :]


def pick_kernel(begin, wanted, features, packed, table, rows, *lists, stride, part, piece):
    feat, nodes = features.shape
    peers, whole, _ = packed.shape
    tucked = part - whole
    buffers, sems = lists[:-1], lists[-1]
    depth = len(buffers)
    exact = buffers[0].shape[0] == part
    skip = 0 if exact else begin[0] % buffers[0].shape[0]

    def fetch(peer, turn):
        first = pl.multiple_of(peer * stride + begin[0] - skip, LANES)
        source = wanted.at[pl.ds(first, buffers[turn].shape[0])]
        return pltpu.make_async_copy(source, buffers[turn], sems.at[turn])

    def one_peer(peer, buffer):
        copy_rows(buffer, table, rows, part, skip)
        if tucked:
            lane = lax.broadcasted_iota(jnp.int32, (tucked, LANES), 1)
            spare = (lane >= feat) & (lane < feat + piece)
            extra = rows[whole:, :]
            for rank in range(4):
                first = rank * tucked
                moved = pltpu.roll(extra, feat - rank * piece, axis=1)
                rows[first : first + tucked, :] = jnp.where(
                    spare, moved, rows[first : first + tucked, :]
                )
        packed[peer] = rows[:whole, :].astype(packed.dtype)

    for turn in range(depth):
        fetch(turn, turn).start()

    table[...] = jnp.zeros(table.shape, jnp.float32)
    for first in range(0, nodes, LANES):
        last = min(first + LANES, nodes)
        table[first:last, :feat] = features[:, first:last].astype(jnp.float32).T

    @pl.loop(0, peers // depth)
    def _(group):
        for turn in range(depth):
            peer = group * depth + turn
            fetch(peer, turn).wait()
            one_peer(peer, buffers[turn])

            @pl.when(peer + depth < peers)
            def _():
                fetch(peer + depth, turn).start()


def pick_rows(wanted, begin, features, peers, part, capacity):
    stride = wanted.shape[0] // peers
    feat, nodes = features.shape
    whole, _, piece = spare_split(part, feat)
    fetched = part if part % LANES == 0 else capacity
    depth = math.gcd(DEPTH, peers)
    return pl.pallas_call(
        functools.partial(pick_kernel, stride=stride, part=part, piece=piece),
        in_specs=[
            pl.BlockSpec(memory_space=pltpu.SMEM),
            pl.BlockSpec(memory_space=pltpu.VMEM),
            pl.BlockSpec(memory_space=pltpu.VMEM),
        ],
        out_specs=pl.BlockSpec(memory_space=pltpu.VMEM),
        scratch_shapes=[
            pltpu.VMEM((nodes, LANES), jnp.float32),
            pltpu.VMEM((part, LANES), jnp.float32),
        ]
        + [pltpu.SMEM((fetched,), jnp.int32)] * depth
        + [pltpu.SemaphoreType.DMA((depth,))],
        out_shape=jax.ShapeDtypeStruct((peers, whole, LANES), features.dtype),
        name="pick",
    )(jnp.reshape(begin, (1,)).astype(jnp.int32), here(wanted), here(features))


def unpack(packed, table, start, whole, capacity, piece, feat):
    tucked = capacity - whole

    @pl.loop(0, packed.shape[0])
    def _(owner):
        base = pl.multiple_of(start + owner * capacity, 8)
        sent = packed[owner].astype(jnp.float32)
        table[pl.ds(base, whole), :] = sent
        if tucked:
            lane = lax.broadcasted_iota(jnp.int32, (tucked, LANES), 1)
            extra = jnp.zeros((tucked, LANES), jnp.float32)
            for part in range(4):
                moved = pltpu.roll(
                    sent[part * tucked : (part + 1) * tucked],
                    (LANES - feat + part * piece) % LANES,
                    axis=1,
                )
                extra = jnp.where(
                    (lane >= part * piece) & (lane < (part + 1) * piece), moved, extra
                )
            table[pl.ds(base + whole, tucked), :] = extra


def project(rows, weight, scores, zvals, sums, heads):
    zvals[...] = jnp.dot(
        rows[...].astype(jnp.bfloat16), weight[...], preferred_element_type=jnp.float32
    ).astype(jnp.bfloat16)
    parts = lax.dot_general(
        zvals[...], scores[...], (((1,), (1,)), ((), ())), preferred_element_type=jnp.float32
    )
    sums[...] = (
        parts
        + pltpu.roll(parts, LANES - heads, axis=1)
        + pltpu.roll(parts, LANES - 2 * heads, axis=1)
    )


def combine(zvals, sums, live, hidden, tie, first, heads, block, slot_total):
    group = min(GROUP, block)
    width = zvals.shape[1]
    lane = lax.broadcasted_iota(jnp.int32, (group, LANES), 1)
    picks = [(lane + column * LANES) // (width // heads) for column in range(width // LANES)]
    for start in range(0, block, group):
        dst = pltpu.roll(sums[start : start + group, :], LANES - 3 * heads, axis=1)
        dst = dst + 0.0 * tie[start : start + group, :]
        alive = live[pl.ds(pl.multiple_of(first + start, 8), group), :]
        logits = []
        for slot in range(slot_total):
            logit = sums[slot * block + start : slot * block + start + group, :] + dst
            logit = jnp.maximum(logit, 0.2 * logit)
            logits.append(jnp.where(alive > slot, logit, -1e30))
        peak = functools.reduce(jnp.maximum, logits)
        shares = [jnp.exp(logit - peak) for logit in logits]
        scale = 1.0 / functools.reduce(jnp.add, shares)
        summed = [None] * len(picks)
        for slot in range(slot_total):
            alpha = (shares[slot] * scale).astype(jnp.bfloat16).astype(jnp.float32)
            for column, pick in enumerate(picks):
                wide = jnp.take_along_axis(alpha, pick, axis=1)
                values = zvals[
                    slot * block + start : slot * block + start + group,
                    column * LANES : (column + 1) * LANES,
                ].astype(jnp.float32)
                term = wide * values
                summed[column] = term if summed[column] is None else summed[column] + term
        for column, total in enumerate(summed):
            low = jnp.minimum(total, 0.0)
            series = low * (1.0 + low * (0.5 + low * (1.0 / 6.0)))
            below = jnp.where(low > -0.01, series, jnp.exp(low) - 1.0)
            hidden[
                pl.ds(pl.multiple_of(first + start, 8), group),
                column * LANES : (column + 1) * LANES,
            ] = jnp.where(total > 0, total, below)


def attend_kernel(
    *refs, near_total, whole, part_whole, capacity, part, piece, feat, heads, block, slot_total
):
    slots, shared, counts, out_weight, far = refs[:5]
    nears = refs[5 : 5 + near_total]
    (
        out, table, rows_even, rows_odd, z_even, z_odd, sums_even, sums_odd, hidden,
        raw, weight, scores, live, even, odd, sems,
    ) = refs[5 + near_total :]
    dst_rows, width = hidden.shape
    blocks = dst_rows // block
    count = block * slot_total
    rows, z, sums = (rows_even, rows_odd), (z_even, z_odd), (sums_even, sums_odd)
    lists = (even, odd)

    def fetch(number, turn):
        source = slots.at[pl.ds(jnp.minimum(number, blocks - 1) * count, count)]
        return pltpu.make_async_copy(source, lists[turn], sems.at[turn])

    fetch(0, 0).start()
    fetch(1, 1).start()

    raw[...] = jnp.zeros(raw.shape, jnp.float32)
    scores[...] = jnp.zeros(scores.shape, scores.dtype)
    side_width = shared.shape[2]
    for side in range(shared.shape[0]):
        raw[: shared.shape[1], side * side_width : (side + 1) * side_width] = shared[
            side
        ].astype(jnp.float32)
    row = lax.broadcasted_iota(jnp.int32, (LANES, width), 0)
    owner = lax.broadcasted_iota(jnp.int32, (LANES, width), 1) // (width // heads)
    weight[...] = jnp.where(row < feat, raw[...], 0.0).astype(jnp.bfloat16)
    lines = [
        jnp.where(
            row[:heads] == owner[:heads],
            jnp.broadcast_to(raw[feat + rank : feat + rank + 1, :], (heads, width)),
            0.0,
        )
        for rank in range(6)
    ]
    scores[: 6 * heads, :] = jnp.concatenate(lines, axis=0).astype(jnp.bfloat16)
    live[...] = jnp.broadcast_to(counts[...], (LANES, dst_rows)).T

    owners = far.shape[0]
    base = 0
    for near in nears:
        unpack(near, table, base, part_whole, part, piece, feat)
        base += owners * part
    unpack(far, table, base, whole, capacity, piece, feat)

    def first_stage(turn):
        project(rows[turn], weight, scores, z[turn], sums[turn], heads)

    fetch(0, 0).wait()
    copy_rows(even, table, rows_even, count)
    first_stage(0)
    fetch(2, 0).start()

    @pl.loop(0, blocks // 2)
    def _(pair):
        for turn in range(2):
            number = 2 * pair + turn
            first = pl.multiple_of(number * block, 8)
            fetch(number + 1, 1 - turn).wait()
            copy_rows(lists[1 - turn], table, rows[1 - turn], count)
            first_stage(1 - turn)
            combine(
                z[turn], sums[turn], live, hidden, rows[1 - turn], first, heads, block, slot_total
            )
            fetch(number + 3, 1 - turn).start()

    fetch(0, 0).wait()
    fetch(0, 1).wait()
    out[...] = jnp.dot(
        hidden[...].astype(jnp.bfloat16), out_weight[...], preferred_element_type=jnp.float32
    ).astype(out.dtype)


def attend(slots, shared, counts, out_weight, far, nears, capacity, part, feat, heads, block):
    whole, _, piece = spare_split(capacity, feat)
    part_whole, _, _ = spare_split(part, feat)
    dst_rows = counts.shape[1]
    slot_total = slots.shape[0] // dst_rows
    width = out_weight.shape[0]
    count = block * slot_total
    return pl.pallas_call(
        functools.partial(
            attend_kernel,
            near_total=len(nears),
            whole=whole,
            part_whole=part_whole,
            capacity=capacity,
            part=part,
            piece=piece,
            feat=feat,
            heads=heads,
            block=block,
            slot_total=slot_total,
        ),
        in_specs=[pl.BlockSpec(memory_space=pl.ANY)]
        + [pl.BlockSpec(memory_space=pltpu.VMEM)] * (4 + len(nears)),
        out_specs=pl.BlockSpec(memory_space=pltpu.VMEM),
        scratch_shapes=[
            pltpu.VMEM((2 * far.shape[0] * capacity, LANES), jnp.float32),
            pltpu.VMEM((count, LANES), jnp.float32),
            pltpu.VMEM((count, LANES), jnp.float32),
            pltpu.VMEM((count, width), jnp.bfloat16),
            pltpu.VMEM((count, width), jnp.bfloat16),
            pltpu.VMEM((count, LANES), jnp.float32),
            pltpu.VMEM((count, LANES), jnp.float32),
            pltpu.VMEM((dst_rows, width), jnp.float32),
            pltpu.VMEM((LANES, width), jnp.float32),
            pltpu.VMEM((LANES, width), jnp.bfloat16),
            pltpu.VMEM((LANES, width), jnp.bfloat16),
            pltpu.VMEM((dst_rows, LANES), jnp.float32),
            pltpu.SMEM((count,), jnp.int32),
            pltpu.SMEM((count,), jnp.int32),
            pltpu.SemaphoreType.DMA((2,)),
        ],
        out_shape=jax.ShapeDtypeStruct((dst_rows, out_weight.shape[1]), jnp.bfloat16),
        name="attend",
    )(slots, *[here(values) for values in (shared, counts, out_weight, far, *nears)])


def three_pieces(values):
    high = lax.reduce_precision(values, 8, 7)
    rest = values - high
    middle = lax.reduce_precision(rest, 8, 7)
    return [piece.astype(jnp.bfloat16) for piece in (high, middle, rest - middle)]


def shared_weights(proj_weight, score_src, score_dst):
    pieces = [
        piece.reshape(1, -1) for score in (score_src, score_dst) for piece in three_pieces(score)
    ]
    mine = jnp.concatenate([proj_weight] + pieces, axis=0)
    if lax.axis_size("head") != 2:
        return lax.all_gather(mine, "head", axis=0, tiled=False)
    turned = [mine] + passed_round(mine)
    side = lax.axis_index("head")
    return jnp.stack([jnp.where(side == rank, turned[0], turned[1]) for rank in range(2)])


def passed_round(values):
    sides = lax.axis_size("head")
    return [
        lax.ppermute(values, "head", [(i, (i + step) % sides) for i in range(sides)])
        for step in range(1, sides)
    ]


def local(
    features, proj_weight, score_src, score_dst, request_rows, slot_index, slot_count, out_weight
):
    groups = lax.axis_size("node")
    half = groups // 2
    upper = lax.axis_index("node") // half
    halves = [list(range(half)), list(range(half, groups))]
    sides = lax.axis_size("head")
    side = lax.axis_index("head")
    capacity = request_rows.shape[2]
    feat = features.shape[1]
    slot_total = slot_index.shape[1]
    dst_rows = slot_index.shape[0] // sides
    block = min(32, dst_rows // 2)

    own = features.T
    across = lax.ppermute(own, "node", [(i, (i + half) % groups) for i in range(groups)])

    def within(values):
        return lax.all_to_all(
            values, "node", split_axis=0, concat_axis=0, axis_index_groups=halves, tiled=True
        )

    part = capacity // sides
    requests = request_rows.reshape(2, half, capacity)
    requests = jnp.where(upper == 0, requests, requests[::-1])
    requests = jnp.transpose(requests, (1, 0, 2))
    wanted = within(requests.reshape(half, 2 * capacity // LANES, LANES)).reshape(-1)

    picked = pick_rows(wanted, side * part, own, half, part, capacity)
    nears = [within(picked)]
    picked = pick_rows(wanted, capacity, across, half, capacity, capacity)
    far = within(picked)
    nears += passed_round(nears[0])

    shared = shared_weights(proj_weight, score_src, score_dst)
    heads = score_src.shape[0] * sides
    slots = lax.dynamic_slice_in_dim(slot_index, side * dst_rows, dst_rows, 0)
    owner, place = slots // capacity, slots % capacity
    peer = owner % half
    turn = (side - place // part) % sides
    slots = jnp.where(
        owner // half == upper,
        (turn * half + peer) * part + place % part,
        (half + peer) * capacity + place,
    )
    slots = jnp.transpose(
        slots.reshape(dst_rows // block, block, slot_total), (0, 2, 1)
    ).reshape(-1)
    counts = lax.dynamic_slice_in_dim(slot_count, side * dst_rows, dst_rows, 0)
    counts = counts.astype(jnp.float32)[None, :]
    return attend(
        slots, shared, counts, out_weight, far, nears, capacity, part, feat, heads, block
    )


def solution(mesh):
    in_specs = (
        P("node", None),
        P(None, "head"),
        P("head", None),
        P("head", None),
        P("node", None, None),
        P("node", None),
        P("node"),
        P(),
    )
    out_specs = P(("node", "head"), None)
    return jax.shard_map(local, mesh=mesh, in_specs=in_specs, out_specs=out_specs, check_vma=False)
```

profile of v0, /device:TPU:0, one launch (start us, length us, event | category | flops | bytes accessed | tf_op | source)
XLA Modules:
  0.0 76.4 jit_solution(5572701966732309139)
XLA Ops:
  0.0 0.8 copy-done.2
  0.8 0.2 rev.3
  1.0 0.6 reshape.45
  1.7 5.3 %all-to-all-start = ((s32[8,8,128]{2,1,0:T(8,128)}), s32[8,8,128]{2,1,0:T(8,128)S(1)}, u32[]{:S(2)}, u32[]{:S(2)}) async-start(s32[8,8,128]{2,1,0:T(8,128)} %reshape.45), calls=%async_computation | async-start | bytes 65536 | tf_op jit(solution)/shard_map/all_to_all | solution.py:352
  6.9 4.8 %all-to-all-done = s32[8,8,128]{2,1,0:T(8,128)S(1)} async-done(((s32[8,8,128]{2,1,0:T(8,128)}), s32[8,8,128]{2,1,0:T(8,128)S(1)}, u32[]{:S(2)}, u32[]{:S(2)}) %all-to-all-start) | async-done | bytes 32800 | tf_op jit(solution)/shard_map/all_to_all | solution.py:352
  11.7 1.0 %copy-done.1 = bf16[2048,100]{0,1:T(8,128)(2,1)S(1)} copy-done((bf16[2048,100]{0,1:T(8,128)(2,1)S(1)}, bf16[2048,100]{0,1:T(8,128)(2,1)}, u32[]{:S(2)}) %copy-start.1) | copy-done | bytes 409624
  12.7 3.0 %pick.3 = bf16[8,208,128]{2,1,0:T(8,128)(2,1)} custom-call(s32[1]{0:T(128)} %bitcast.8.begin, s32[8192]{0:T(1024)S(1)} %bitcast.18, bf16[100,2048]{1,0:T(8,128)(2,1)S(1)} %bitcast.16), custom_call_target="tpu_custom_call" | custom-call | tf_op jit(solution)/shard_map/pick/pallas_call | solution.py:88
  15.7 3.5 %all-to-all-start.2 = ((bf16[8,208,128]{2,1,0:T(8,128)(2,1)}), bf16[8,208,128]{2,1,0:T(8,128)(2,1)S(1)}, u32[]{:S(2)}, u32[]{:S(2)}) async-start(bf16[8,208,128]{2,1,0:T(8,128)(2,1)} %pick.3), calls=%async_computation.2 | async-start | bytes 851968 | tf_op jit(solution)/shard_map/all_to_all | solution.py:352
  19.2 2.7 %collective-permute-start.1 = (bf16[100,2048]{1,0:T(8,128)(2,1)S(1)}, bf16[100,2048]{1,0:T(8,128)(2,1)S(1)}, u32[]{:S(2)}, u32[]{:S(2)}) collective-permute-start(bf16[100,2048]{1,0:T(8,128)(2,1)S(1)} %bitcast.17), channel_id=1, source_target_pairs={{0,16},{2,18},{4,20},{6,22},{8,24},{10,26},{12,28},{14,30},{16,0},... | collective-permute-start | bytes 1228808 | tf_op jit(solution)/shard_map/ppermute | solution.py:349
  21.9 19.5 %collective-permute-done.1.features = bf16[100,2048]{1,0:T(8,128)(2,1)S(1)} collective-permute-done((bf16[100,2048]{1,0:T(8,128)(2,1)S(1)}, bf16[100,2048]{1,0:T(8,128)(2,1)S(1)}, u32[]{:S(2)}, u32[]{:S(2)}) %collective-permute-start.1) | collective-permute-done | bytes 409632 | tf_op jit(solution)/shard_map/ppermute | solution.py:349
  41.4 4.9 %pick.2 = bf16[8,416,128]{2,1,0:T(8,128)(2,1)} custom-call(s32[1]{0:T(128)} %constant.100.clone.1.begin, s32[8192]{0:T(1024)S(1)} %bitcast.19, bf16[100,2048]{1,0:T(8,128)(2,1)S(1)} %collective-permute-done.1.features), custom_call_target="tpu_custom_call" | custom-call | tf_op jit(solution)/shard_map/pick/pallas_call | solution.py:88
  46.4 3.7 %all-to-all-start.1 = ((bf16[8,416,128]{2,1,0:T(8,128)(2,1)}), bf16[8,416,128]{2,1,0:T(8,128)(2,1)S(1)}, u32[]{:S(2)}, u32[]{:S(2)}) async-start(bf16[8,416,128]{2,1,0:T(8,128)(2,1)} %pick.2), calls=%async_computation.1 | async-start | bytes 1703936 | tf_op jit(solution)/shard_map/all_to_all | solution.py:352
  50.1 0.1 reshape.38
  50.2 0.1 reshape.39
  50.3 0.1 reshape.40
  50.3 0.1 reshape.41
  50.4 0.1 reshape.42
  50.5 0.1 reshape.43
  50.7 1.6 %collective-permute-start = (bf16[106,256]{1,0:T(8,128)(2,1)S(1)}, bf16[106,256]{1,0:T(8,128)(2,1)S(1)}, u32[]{:S(2)}, u32[]{:S(2)}) collective-permute-start(bf16[106,256]{1,0:T(8,128)(2,1)S(1)} %concatenate.3), channel_id=1, source_target_pairs={{0,1},{1,0},{2,3},{3,2},{4,5},{5,4},{6,7},{7,6},{8,9},{9,8},{10,11... | collective-permute-start | bytes 162824 | tf_op jit(solution)/shard_map/ppermute | solution.py:328
  52.3 0.6 collective-permute-start.2
  53.0 0.7 reshape.37.refs_0_
  53.7 1.2 %collective-permute-done = bf16[106,256]{1,0:T(8,128)(2,1)S(1)} collective-permute-done((bf16[106,256]{1,0:T(8,128)(2,1)S(1)}, bf16[106,256]{1,0:T(8,128)(2,1)S(1)}, u32[]{:S(2)}, u32[]{:S(2)}) %collective-permute-start) | collective-permute-done | bytes 54304 | tf_op jit(solution)/shard_map/ppermute | solution.py:328
  54.9 9.2 %collective-permute-done.2.refs_6_ = bf16[8,208,128]{2,1,0:T(8,128)(2,1)S(1)} collective-permute-done((bf16[8,208,128]{2,1,0:T(8,128)(2,1)S(1)}, bf16[8,208,128]{2,1,0:T(8,128)(2,1)S(1)}, u32[]{:S(2)}, u32[]{:S(2)}) %collective-permute-start.2) | collective-permute-done | bytes 426016 | tf_op jit(solution)/shard_map/ppermute | solution.py:328
  64.2 12.2 %attend.1 = bf16[256,512]{1,0:T(8,128)(2,1)} custom-call(s32[4096]{0:T(1024)} %reshape.37.refs_0_, bf16[2,106,256]{2,1,0:T(8,128)(2,1)S(1)} %pad_maximum_fusion.refs_1_, f32[1,256]{1,0:T(1,128)S(1)} %bitcast.20, bf16[512,512]{1,0:T(8,128)(2,1)S(1)} %copy-done, bf16[8,416,128]{2,1,0:T(8,128)(2,1)S(1)} %all-to-all-done.1.refs_4_, ...), custom_call_target="tpu_custom_call" | custom-call | tf_op jit(solution)/shard_map/attend/pallas_call | solution.py:267
  (27 shorter events, 0.4 us)
Async XLA Ops:
  0.0 0.8 copy-start.2
  1.7 10.0 %all-to-all-start = ((s32[8,8,128]{2,1,0:T(8,128)}), s32[8,8,128]{2,1,0:T(8,128)S(1)}, u32[]{:S(2)}, u32[]{:S(2)}) async-start(s32[8,8,128]{2,1,0:T(8,128)} %reshape.45), calls=%async_computation | async-start | bytes 65536 | tf_op jit(solution)/shard_map/all_to_all | solution.py:352
  11.7 1.0 %copy-start.1 = (bf16[2048,100]{0,1:T(8,128)(2,1)S(1)}, bf16[2048,100]{0,1:T(8,128)(2,1)}, u32[]{:S(2)}) copy-start(bf16[2048,100]{0,1:T(8,128)(2,1)} %param.8) | copy-start | bytes 1228804
  15.7 30.6 %all-to-all-start.2 = ((bf16[8,208,128]{2,1,0:T(8,128)(2,1)}), bf16[8,208,128]{2,1,0:T(8,128)(2,1)S(1)}, u32[]{:S(2)}, u32[]{:S(2)}) async-start(bf16[8,208,128]{2,1,0:T(8,128)(2,1)} %pick.3), calls=%async_computation.2 | async-start | bytes 851968 | tf_op jit(solution)/shard_map/all_to_all | solution.py:352
  19.2 22.2 %collective-permute-start.1 = (bf16[100,2048]{1,0:T(8,128)(2,1)S(1)}, bf16[100,2048]{1,0:T(8,128)(2,1)S(1)}, u32[]{:S(2)}, u32[]{:S(2)}) collective-permute-start(bf16[100,2048]{1,0:T(8,128)(2,1)S(1)} %bitcast.17), channel_id=1, source_target_pairs={{0,16},{2,18},{4,20},{6,22},{8,24},{10,26},{12,28},{14,30},{16,0},... | collective-permute-start | bytes 1228808 | tf_op jit(solution)/shard_map/ppermute | solution.py:349
  46.3 3.8 %copy-start.5 = (f32[4,64]{1,0:T(4,128)S(1)}, f32[4,64]{1,0:T(4,128)}, u32[]{:S(2)}) copy-start(f32[4,64]{1,0:T(4,128)} %param.10) | copy-start | bytes 3076
  46.3 4.0 %copy-start.6 = (f32[4,64]{1,0:T(4,128)S(1)}, f32[4,64]{1,0:T(4,128)}, u32[]{:S(2)}) copy-start(f32[4,64]{1,0:T(4,128)} %param.11) | copy-start | bytes 3076
  46.3 4.3 %copy-start.3 = (bf16[100,256]{1,0:T(8,128)(2,1)S(1)}, bf16[100,256]{1,0:T(8,128)(2,1)}, u32[]{:S(2)}) copy-start(bf16[100,256]{1,0:T(8,128)(2,1)} %param.9) | copy-start | bytes 153604
  46.3 5.9 %copy-start.4 = (s32[512,16]{0,1:T(8,128)S(1)}, s32[512,16]{0,1:T(8,128)}, u32[]{:S(2)}) copy-start(s32[512,16]{0,1:T(8,128)} %param.13) | copy-start | bytes 98308
  46.3 6.5 %copy-start.7 = (s32[512]{0:T(512)S(1)}, s32[512]{0:T(512)}, u32[]{:S(2)}) copy-start(s32[512]{0:T(512)} %param.14) | copy-start | bytes 6148
  46.4 17.8 %all-to-all-start.1 = ((bf16[8,416,128]{2,1,0:T(8,128)(2,1)}), bf16[8,416,128]{2,1,0:T(8,128)(2,1)S(1)}, u32[]{:S(2)}, u32[]{:S(2)}) async-start(bf16[8,416,128]{2,1,0:T(8,128)(2,1)} %pick.2), calls=%async_computation.1 | async-start | bytes 1703936 | tf_op jit(solution)/shard_map/all_to_all | solution.py:352
  50.1 14.1 %copy-start = (bf16[512,512]{1,0:T(8,128)(2,1)S(1)}, bf16[512,512]{1,0:T(8,128)(2,1)}, u32[]{:S(2)}) copy-start(bf16[512,512]{1,0:T(8,128)(2,1)} %refs_3_.1) | copy-start | bytes 1572868
  50.7 4.3 %collective-permute-start = (bf16[106,256]{1,0:T(8,128)(2,1)S(1)}, bf16[106,256]{1,0:T(8,128)(2,1)S(1)}, u32[]{:S(2)}, u32[]{:S(2)}) collective-permute-start(bf16[106,256]{1,0:T(8,128)(2,1)S(1)} %concatenate.3), channel_id=1, source_target_pairs={{0,1},{1,0},{2,3},{3,2},{4,5},{5,4},{6,7},{7,6},{8,9},{9,8},{10,11... | collective-permute-start | bytes 162824 | tf_op jit(solution)/shard_map/ppermute | solution.py:328
  52.3 11.9 %collective-permute-start.2 = (bf16[8,208,128]{2,1,0:T(8,128)(2,1)S(1)}, bf16[8,208,128]{2,1,0:T(8,128)(2,1)S(1)}, u32[]{:S(2)}, u32[]{:S(2)}) collective-permute-start(bf16[8,208,128]{2,1,0:T(8,128)(2,1)S(1)} %all-to-all-done.2.refs_5_), channel_id=1, source_target_pairs={{0,1},{1,0},{2,3},{3,2},{4,5},{5,4},{6,7},{7,6},{8,9},{9,8},{10,11... | collective-permute-start | bytes 1277960 | tf_op jit(solution)/shard_map/ppermute | solution.py:328
where the time goes:
time: 76.9 us; the launch traced here: 76.4 us
  waiting for transfers between devices  34.7 us (45%)
  Pallas kernels  20 us (26%)
  starting transfers between devices  17.2 us (22%)
  local copies, waits for them, and re-layouts  4 us (5%)
    ppermute x1, waiting for transfers between devices, local(): lax.ppermute(own, 'node', [(i, (i + half) % groups) for i in range(groups)])  19.5 us
    all_to_all x3, starting transfers between devices, within(): lax.all_to_all(values, 'node', split_axis=0, concat_axis=0, axis_index_gr...  12.4 us
    pallas_call x1, Pallas kernels, attend(): pl.pallas_call(functools.partial(attend_kernel, near_total=len(nears), wh...  12.2 us
    ppermute x2, waiting for transfers between devices, passed_round(): lax.ppermute(values, 'head', [(i, (i + step) % sides) for i in range(side...  10.4 us
    pallas_call x2, Pallas kernels, pick_rows(): pl.pallas_call(functools.partial(pick_kernel, stride=stride, part=part, p...  7.87 us
    all_to_all x3, waiting for transfers between devices, within(): lax.all_to_all(values, 'node', split_axis=0, concat_axis=0, axis_index_gr...  4.76 us
    ppermute x1, starting transfers between devices, local(): lax.ppermute(own, 'node', [(i, (i + half) % groups) for i in range(groups)])  2.66 us
    ppermute x2, starting transfers between devices, passed_round(): lax.ppermute(values, 'head', [(i, (i + step) % sides) for i in range(side...  2.14 us
  transfers between devices with their start and end apart: 6, of which 4 were waited for; matrix products, arithmetic and copies ran while one was open for 2% of the time, Pallas kernels for 6%

commit v1 on v0

--- a/solution.py
+++ b/solution.py
@@ -101,7 +101,7 @@
         + [pltpu.SemaphoreType.DMA((depth,))],
         out_shape=jax.ShapeDtypeStruct((peers, whole, LANES), features.dtype),
         name="pick",
-    )(jnp.reshape(begin, (1,)).astype(jnp.int32), here(wanted), here(features))
+    )(jnp.reshape(begin, (1,)).astype(jnp.int32), here(wanted), features)
 
 
 def unpack(packed, table, start, whole, capacity, piece, feat):
@@ -312,7 +312,9 @@
 
 def shared_weights(proj_weight, score_src, score_dst):
     pieces = [
-        piece.reshape(1, -1) for score in (score_src, score_dst) for piece in three_pieces(score)
+        piece.reshape(1, -1)
+        for values in (score_src, score_dst)
+        for piece in three_pieces(values)
     ]
     mine = jnp.concatenate([proj_weight] + pieces, axis=0)
     if lax.axis_size("head") != 2:
@@ -361,7 +363,7 @@
 
     picked = pick_rows(wanted, side * part, own, half, part, capacity)
     nears = [within(picked)]
-    picked = pick_rows(wanted, capacity, across, half, capacity, capacity)
+    picked = pick_rows(wanted, capacity, here(across), half, capacity, capacity)
     far = within(picked)
     nears += passed_round(nears[0])
 

time: 76.9 us -> 76.9 us (level)
  local copies, waits for them, and re-layouts: 4 us -> 3 us
  Pallas kernels: 20 us -> 20.9 us
    unnamed x16, local copies, waits for them, and re-layouts: 1.8 us -> 0.8 us
    pallas_call x2, Pallas kernels: 7.87 us -> 8.73 us  [pick_rows(): pl.pallas_call(functools.partial(pick_kernel, stride=stride, part=part, p...]
where the time goes in v1:
time: 76.9 us; the launch traced here: 76.4 us
  waiting for transfers between devices  34.7 us (45%)
  Pallas kernels  20.9 us (27%)
  starting transfers between devices  17.3 us (22%)
  local copies, waits for them, and re-layouts  3 us (4%)
    ppermute x1, waiting for transfers between devices, local(): lax.ppermute(own, 'node', [(i, (i + half) % groups) for i in range(groups)])  19.5 us
    all_to_all x3, starting transfers between devices, within(): lax.all_to_all(values, 'node', split_axis=0, concat_axis=0, axis_index_gr...  12.6 us
    pallas_call x1, Pallas kernels, attend(): pl.pallas_call(functools.partial(attend_kernel, near_total=len(nears), wh...  12.2 us
    ppermute x2, waiting for transfers between devices, passed_round(): lax.ppermute(values, 'head', [(i, (i + step) % sides) for i in range(side...  10.4 us
    pallas_call x2, Pallas kernels, pick_rows(): pl.pallas_call(functools.partial(pick_kernel, stride=stride, part=part, p...  8.73 us
    all_to_all x3, waiting for transfers between devices, within(): lax.all_to_all(values, 'node', split_axis=0, concat_axis=0, axis_index_gr...  4.76 us
    ppermute x1, starting transfers between devices, local(): lax.ppermute(own, 'node', [(i, (i + half) % groups) for i in range(groups)])  2.66 us
    ppermute x2, starting transfers between devices, passed_round(): lax.ppermute(values, 'head', [(i, (i + step) % sides) for i in range(side...  2.14 us
  transfers between devices with their start and end apart: 6, of which 4 were waited for; matrix products, arithmetic and copies ran while one was open for 2% of the time, Pallas kernels for 6%

profile of v1, /device:TPU:0, one launch (start us, length us, event | category | flops | bytes accessed | tf_op | source)
XLA Modules:
  0.0 76.4 jit_solution(2763891931760740262)
XLA Ops:
  0.0 0.8 copy-done.2
  0.8 0.2 rev.3
  1.0 0.6 reshape.45
  1.7 5.3 %all-to-all-start = ((s32[8,8,128]{2,1,0:T(8,128)}), s32[8,8,128]{2,1,0:T(8,128)S(1)}, u32[]{:S(2)}, u32[]{:S(2)}) async-start(s32[8,8,128]{2,1,0:T(8,128)} %reshape.45), calls=%async_computation | async-start | bytes 65536 | tf_op jit(solution)/shard_map/all_to_all | solution.py:354
  6.9 4.8 %all-to-all-done = s32[8,8,128]{2,1,0:T(8,128)S(1)} async-done(((s32[8,8,128]{2,1,0:T(8,128)}), s32[8,8,128]{2,1,0:T(8,128)S(1)}, u32[]{:S(2)}, u32[]{:S(2)}) %all-to-all-start) | async-done | bytes 32800 | tf_op jit(solution)/shard_map/all_to_all | solution.py:354
  11.7 3.9 %pick.3 = bf16[8,208,128]{2,1,0:T(8,128)(2,1)} custom-call(s32[1]{0:T(128)} %bitcast.8.begin, s32[8192]{0:T(1024)S(1)} %bitcast.16, bf16[100,2048]{1,0:T(8,128)(2,1)} %bitcast.19), custom_call_target="tpu_custom_call" | custom-call | tf_op jit(solution)/shard_map/pick/pallas_call | solution.py:88
  15.6 3.6 %all-to-all-start.2 = ((bf16[8,208,128]{2,1,0:T(8,128)(2,1)}), bf16[8,208,128]{2,1,0:T(8,128)(2,1)S(1)}, u32[]{:S(2)}, u32[]{:S(2)}) async-start(bf16[8,208,128]{2,1,0:T(8,128)(2,1)} %pick.3), calls=%async_computation.2 | async-start | bytes 851968 | tf_op jit(solution)/shard_map/all_to_all | solution.py:354
  19.2 2.7 %collective-permute-start.1 = (bf16[100,2048]{1,0:T(8,128)(2,1)S(1)}, bf16[100,2048]{1,0:T(8,128)(2,1)S(1)}, u32[]{:S(2)}, u32[]{:S(2)}) collective-permute-start(bf16[100,2048]{1,0:T(8,128)(2,1)S(1)} %bitcast.20), channel_id=1, source_target_pairs={{0,16},{2,18},{4,20},{6,22},{8,24},{10,26},{12,28},{14,30},{16,0},... | collective-permute-start | bytes 1228808 | tf_op jit(solution)/shard_map/ppermute | solution.py:351
  21.9 19.5 %collective-permute-done.1.features = bf16[100,2048]{1,0:T(8,128)(2,1)S(1)} collective-permute-done((bf16[100,2048]{1,0:T(8,128)(2,1)S(1)}, bf16[100,2048]{1,0:T(8,128)(2,1)S(1)}, u32[]{:S(2)}, u32[]{:S(2)}) %collective-permute-start.1) | collective-permute-done | bytes 409632 | tf_op jit(solution)/shard_map/ppermute | solution.py:351
  41.4 4.9 %pick.2 = bf16[8,416,128]{2,1,0:T(8,128)(2,1)} custom-call(s32[1]{0:T(128)} %constant.100.clone.1.begin, s32[8192]{0:T(1024)S(1)} %bitcast.17, bf16[100,2048]{1,0:T(8,128)(2,1)S(1)} %collective-permute-done.1.features), custom_call_target="tpu_custom_call" | custom-call | tf_op jit(solution)/shard_map/pick/pallas_call | solution.py:88
  46.3 3.7 %all-to-all-start.1 = ((bf16[8,416,128]{2,1,0:T(8,128)(2,1)}), bf16[8,416,128]{2,1,0:T(8,128)(2,1)S(1)}, u32[]{:S(2)}, u32[]{:S(2)}) async-start(bf16[8,416,128]{2,1,0:T(8,128)(2,1)} %pick.2), calls=%async_computation.1 | async-start | bytes 1703936 | tf_op jit(solution)/shard_map/all_to_all | solution.py:354
  50.1 0.1 reshape.38
  50.2 0.1 reshape.39
  50.2 0.1 reshape.40
  50.3 0.1 reshape.41
  50.4 0.1 reshape.42
  50.5 0.1 reshape.43
  50.6 1.6 %collective-permute-start = (bf16[106,256]{1,0:T(8,128)(2,1)S(1)}, bf16[106,256]{1,0:T(8,128)(2,1)S(1)}, u32[]{:S(2)}, u32[]{:S(2)}) collective-permute-start(bf16[106,256]{1,0:T(8,128)(2,1)S(1)} %concatenate.3), channel_id=1, source_target_pairs={{0,1},{1,0},{2,3},{3,2},{4,5},{5,4},{6,7},{7,6},{8,9},{9,8},{10,11... | collective-permute-start | bytes 162824 | tf_op jit(solution)/shard_map/ppermute | solution.py:330
  52.3 0.6 collective-permute-start.2
  52.9 0.1 dynamic-slice_convert_fusion
  53.0 0.7 reshape.37.refs_0_
  53.7 1.2 %collective-permute-done = bf16[106,256]{1,0:T(8,128)(2,1)S(1)} collective-permute-done((bf16[106,256]{1,0:T(8,128)(2,1)S(1)}, bf16[106,256]{1,0:T(8,128)(2,1)S(1)}, u32[]{:S(2)}, u32[]{:S(2)}) %collective-permute-start) | collective-permute-done | bytes 54304 | tf_op jit(solution)/shard_map/ppermute | solution.py:330
  54.9 9.2 %collective-permute-done.2.refs_6_ = bf16[8,208,128]{2,1,0:T(8,128)(2,1)S(1)} collective-permute-done((bf16[8,208,128]{2,1,0:T(8,128)(2,1)S(1)}, bf16[8,208,128]{2,1,0:T(8,128)(2,1)S(1)}, u32[]{:S(2)}, u32[]{:S(2)}) %collective-permute-start.2) | collective-permute-done | bytes 426016 | tf_op jit(solution)/shard_map/ppermute | solution.py:330
  64.2 12.2 %attend.1 = bf16[256,512]{1,0:T(8,128)(2,1)} custom-call(s32[4096]{0:T(1024)} %reshape.37.refs_0_, bf16[2,106,256]{2,1,0:T(8,128)(2,1)S(1)} %pad_maximum_fusion.refs_1_, f32[1,256]{1,0:T(1,128)S(1)} %bitcast.18, bf16[512,512]{1,0:T(8,128)(2,1)S(1)} %copy-done, bf16[8,416,128]{2,1,0:T(8,128)(2,1)S(1)} %all-to-all-done.1.refs_4_, ...), custom_call_target="tpu_custom_call" | custom-call | tf_op jit(solution)/shard_map/attend/pallas_call | solution.py:267
  (27 shorter events, 0.4 us)
Async XLA Ops:
  0.0 0.8 copy-start.2
  1.7 10.0 %all-to-all-start = ((s32[8,8,128]{2,1,0:T(8,128)}), s32[8,8,128]{2,1,0:T(8,128)S(1)}, u32[]{:S(2)}, u32[]{:S(2)}) async-start(s32[8,8,128]{2,1,0:T(8,128)} %reshape.45), calls=%async_computation | async-start | bytes 65536 | tf_op jit(solution)/shard_map/all_to_all | solution.py:354
  15.6 3.6 %copy-start.1 = (bf16[2048,100]{0,1:T(8,128)(2,1)S(1)}, bf16[2048,100]{0,1:T(8,128)(2,1)}, u32[]{:S(2)}) copy-start(bf16[2048,100]{0,1:T(8,128)(2,1)} %param.8) | copy-start | bytes 1228804
  15.6 30.7 %all-to-all-start.2 = ((bf16[8,208,128]{2,1,0:T(8,128)(2,1)}), bf16[8,208,128]{2,1,0:T(8,128)(2,1)S(1)}, u32[]{:S(2)}, u32[]{:S(2)}) async-start(bf16[8,208,128]{2,1,0:T(8,128)(2,1)} %pick.3), calls=%async_computation.2 | async-start | bytes 851968 | tf_op jit(solution)/shard_map/all_to_all | solution.py:354
  19.2 22.2 %collective-permute-start.1 = (bf16[100,2048]{1,0:T(8,128)(2,1)S(1)}, bf16[100,2048]{1,0:T(8,128)(2,1)S(1)}, u32[]{:S(2)}, u32[]{:S(2)}) collective-permute-start(bf16[100,2048]{1,0:T(8,128)(2,1)S(1)} %bitcast.20), channel_id=1, source_target_pairs={{0,16},{2,18},{4,20},{6,22},{8,24},{10,26},{12,28},{14,30},{16,0},... | collective-permute-start | bytes 1228808 | tf_op jit(solution)/shard_map/ppermute | solution.py:351
  46.3 3.8 %copy-start.5 = (f32[4,64]{1,0:T(4,128)S(1)}, f32[4,64]{1,0:T(4,128)}, u32[]{:S(2)}) copy-start(f32[4,64]{1,0:T(4,128)} %param.10) | copy-start | bytes 3076
  46.3 4.0 %copy-start.6 = (f32[4,64]{1,0:T(4,128)S(1)}, f32[4,64]{1,0:T(4,128)}, u32[]{:S(2)}) copy-start(f32[4,64]{1,0:T(4,128)} %param.11) | copy-start | bytes 3076
  46.3 4.3 %copy-start.3 = (bf16[100,256]{1,0:T(8,128)(2,1)S(1)}, bf16[100,256]{1,0:T(8,128)(2,1)}, u32[]{:S(2)}) copy-start(bf16[100,256]{1,0:T(8,128)(2,1)} %param.9) | copy-start | bytes 153604
  46.3 5.9 %copy-start.4 = (s32[512,16]{0,1:T(8,128)S(1)}, s32[512,16]{0,1:T(8,128)}, u32[]{:S(2)}) copy-start(s32[512,16]{0,1:T(8,128)} %param.13) | copy-start | bytes 98308
  46.3 6.5 %copy-start.7 = (s32[512]{0:T(512)S(1)}, s32[512]{0:T(512)}, u32[]{:S(2)}) copy-start(s32[512]{0:T(512)} %param.14) | copy-start | bytes 6148
  46.3 17.8 %all-to-all-start.1 = ((bf16[8,416,128]{2,1,0:T(8,128)(2,1)}), bf16[8,416,128]{2,1,0:T(8,128)(2,1)S(1)}, u32[]{:S(2)}, u32[]{:S(2)}) async-start(bf16[8,416,128]{2,1,0:T(8,128)(2,1)} %pick.2), calls=%async_computation.1 | async-start | bytes 1703936 | tf_op jit(solution)/shard_map/all_to_all | solution.py:354
  50.1 14.1 %copy-start = (bf16[512,512]{1,0:T(8,128)(2,1)S(1)}, bf16[512,512]{1,0:T(8,128)(2,1)}, u32[]{:S(2)}) copy-start(bf16[512,512]{1,0:T(8,128)(2,1)} %refs_3_.1) | copy-start | bytes 1572868
  50.6 4.3 %collective-permute-start = (bf16[106,256]{1,0:T(8,128)(2,1)S(1)}, bf16[106,256]{1,0:T(8,128)(2,1)S(1)}, u32[]{:S(2)}, u32[]{:S(2)}) collective-permute-start(bf16[106,256]{1,0:T(8,128)(2,1)S(1)} %concatenate.3), channel_id=1, source_target_pairs={{0,1},{1,0},{2,3},{3,2},{4,5},{5,4},{6,7},{7,6},{8,9},{9,8},{10,11... | collective-permute-start | bytes 162824 | tf_op jit(solution)/shard_map/ppermute | solution.py:330
  52.3 11.9 %collective-permute-start.2 = (bf16[8,208,128]{2,1,0:T(8,128)(2,1)S(1)}, bf16[8,208,128]{2,1,0:T(8,128)(2,1)S(1)}, u32[]{:S(2)}, u32[]{:S(2)}) collective-permute-start(bf16[8,208,128]{2,1,0:T(8,128)(2,1)S(1)} %all-to-all-done.2.refs_5_), channel_id=1, source_target_pairs={{0,1},{1,0},{2,3},{3,2},{4,5},{5,4},{6,7},{7,6},{8,9},{9,8},{10,11... | collective-permute-start | bytes 1277960 | tf_op jit(solution)/shard_map/ppermute | solution.py:330

commit v2 on v1

--- a/solution.py
+++ b/solution.py
@@ -127,14 +127,14 @@
             table[pl.ds(base + whole, tucked), :] = extra
 
 
-def project(rows, weight, scores, zvals, sums, heads):
-    zvals[...] = jnp.dot(
-        rows[...].astype(jnp.bfloat16), weight[...], preferred_element_type=jnp.float32
+def project(rows, weight, scores, zvals, sums, heads, count):
+    zvals[:count, :] = jnp.dot(
+        rows[:count, :].astype(jnp.bfloat16), weight[...], preferred_element_type=jnp.float32
     ).astype(jnp.bfloat16)
     parts = lax.dot_general(
-        zvals[...], scores[...], (((1,), (1,)), ((), ())), preferred_element_type=jnp.float32
-    )
-    sums[...] = (
+        zvals[:count, :], scores[...], (((1,), (1,)), ((), ())), preferred_element_type=jnp.float32
+    )
+    sums[:count, :] = (
         parts
         + pltpu.roll(parts, LANES - heads, axis=1)
         + pltpu.roll(parts, LANES - 2 * heads, axis=1)
@@ -180,14 +180,14 @@
 
 
 def attend_kernel(
-    *refs, near_total, whole, part_whole, capacity, part, piece, feat, heads, block, slot_total
+    *refs, near_total, whole, part_whole, capacity, part, piece, feat, heads, block, slot_total, step
 ):
-    slots, shared, counts, out_weight, far = refs[:5]
-    nears = refs[5 : 5 + near_total]
+    slots, levels, shared, counts, ranks, out_weight, far = refs[:7]
+    nears = refs[7 : 7 + near_total]
     (
         out, table, rows_even, rows_odd, z_even, z_odd, sums_even, sums_odd, hidden,
-        raw, weight, scores, live, even, odd, sems,
-    ) = refs[5 + near_total :]
+        raw, weight, scores, live, back, even, odd, sems,
+    ) = refs[7 + near_total :]
     dst_rows, width = hidden.shape
     blocks = dst_rows // block
     count = block * slot_total
@@ -229,12 +229,17 @@
         base += owners * part
     unpack(far, table, base, whole, capacity, piece, feat)
 
-    def first_stage(turn):
-        project(rows[turn], weight, scores, z[turn], sums[turn], heads)
+    place = lax.broadcasted_iota(jnp.int32, (dst_rows, dst_rows), 0).astype(jnp.float32)
+    back[...] = jnp.where(
+        jnp.broadcast_to(ranks[...], (dst_rows, dst_rows)) == place, 1.0, 0.0
+    ).T.astype(jnp.bfloat16)
+
+    def first_stage(turn, count):
+        project(rows[turn], weight, scores, z[turn], sums[turn], heads, count)
 
     fetch(0, 0).wait()
     copy_rows(even, table, rows_even, count)
-    first_stage(0)
+    first_stage(0, count)
     fetch(2, 0).start()
 
     @pl.loop(0, blocks // 2)
@@ -242,22 +247,34 @@
         for turn in range(2):
             number = 2 * pair + turn
             first = pl.multiple_of(number * block, 8)
+            level = levels[number]
             fetch(number + 1, 1 - turn).wait()
-            copy_rows(lists[1 - turn], table, rows[1 - turn], count)
-            first_stage(1 - turn)
-            combine(
-                z[turn], sums[turn], live, hidden, rows[1 - turn], first, heads, block, slot_total
-            )
+            for used in range(step, slot_total + 1, step):
+
+                @pl.when(level == used // step)
+                def _(turn=turn, used=used, first=first):
+                    copy_rows(lists[1 - turn], table, rows[1 - turn], block * used)
+                    first_stage(1 - turn, block * used)
+                    combine(
+                        z[turn], sums[turn], live, hidden, rows[1 - turn], first, heads, block, used
+                    )
+
             fetch(number + 3, 1 - turn).start()
 
     fetch(0, 0).wait()
     fetch(0, 1).wait()
-    out[...] = jnp.dot(
-        hidden[...].astype(jnp.bfloat16), out_weight[...], preferred_element_type=jnp.float32
-    ).astype(out.dtype)
-
-
-def attend(slots, shared, counts, out_weight, far, nears, capacity, part, feat, heads, block):
+    ordered = jnp.dot(
+        back[...], hidden[...].astype(jnp.bfloat16), preferred_element_type=jnp.float32
+    ).astype(jnp.bfloat16)
+    out[...] = jnp.dot(ordered, out_weight[...], preferred_element_type=jnp.float32).astype(
+        out.dtype
+    )
+
+
+def attend(
+    slots, levels, shared, counts, ranks, out_weight, far, nears,
+    capacity, part, feat, heads, block, step
+):
     whole, _, piece = spare_split(capacity, feat)
     part_whole, _, _ = spare_split(part, feat)
     dst_rows = counts.shape[1]
@@ -277,9 +294,10 @@
             heads=heads,
             block=block,
             slot_total=slot_total,
+            step=step,
         ),
-        in_specs=[pl.BlockSpec(memory_space=pl.ANY)]
-        + [pl.BlockSpec(memory_space=pltpu.VMEM)] * (4 + len(nears)),
+        in_specs=[pl.BlockSpec(memory_space=pl.ANY), pl.BlockSpec(memory_space=pltpu.SMEM)]
+        + [pl.BlockSpec(memory_space=pltpu.VMEM)] * (5 + len(nears)),
         out_specs=pl.BlockSpec(memory_space=pltpu.VMEM),
         scratch_shapes=[
             pltpu.VMEM((2 * far.shape[0] * capacity, LANES), jnp.float32),
@@ -294,13 +312,16 @@
             pltpu.VMEM((LANES, width), jnp.bfloat16),
             pltpu.VMEM((LANES, width), jnp.bfloat16),
             pltpu.VMEM((dst_rows, LANES), jnp.float32),
+            pltpu.VMEM((dst_rows, dst_rows), jnp.bfloat16),
             pltpu.SMEM((count,), jnp.int32),
             pltpu.SMEM((count,), jnp.int32),
             pltpu.SemaphoreType.DMA((2,)),
         ],
         out_shape=jax.ShapeDtypeStruct((dst_rows, out_weight.shape[1]), jnp.bfloat16),
         name="attend",
-    )(slots, *[here(values) for values in (shared, counts, out_weight, far, *nears)])
+    )(
+        slots, levels, *[here(values) for values in (shared, counts, ranks, out_weight, far, *nears)]
+    )
 
 
 def three_pieces(values):
@@ -330,6 +351,20 @@
         lax.ppermute(values, "head", [(i, (i + step) % sides) for i in range(sides)])
         for step in range(1, sides)
     ]
+
+
+def by_count(slots, counts):
+    rows = counts.shape[0]
+    order = jnp.arange(rows, dtype=jnp.int32)
+    same = (counts[None, :] == counts[:, None]) & (order[None, :] < order[:, None])
+    ahead = (counts[None, :] > counts[:, None]) | same
+    ranks = jnp.sum(ahead.astype(jnp.int32), axis=1)
+    hot = (ranks[None, :] == order[:, None]).astype(jnp.bfloat16)
+    digits = [slots // 65536, slots // 256 % 256, slots % 256, counts[:, None]]
+    digits = jnp.concatenate(digits, axis=1).astype(jnp.bfloat16)
+    moved = jnp.dot(hot, digits, preferred_element_type=jnp.float32).astype(jnp.int32)
+    high, middle, low, last = jnp.split(moved, [slots.shape[1] * k for k in (1, 2, 3)], axis=1)
+    return high * 65536 + middle * 256 + low, last[:, 0], ranks
 
 
 def local(
@@ -378,13 +413,18 @@
         (turn * half + peer) * part + place % part,
         (half + peer) * capacity + place,
     )
+    counts = lax.dynamic_slice_in_dim(slot_count, side * dst_rows, dst_rows, 0)
+    slots, counts, ranks = by_count(slots, counts)
+    step = slot_total // 4 if slot_total % 4 == 0 else slot_total
+    levels = (counts[::block] + step - 1) // step
     slots = jnp.transpose(
         slots.reshape(dst_rows // block, block, slot_total), (0, 2, 1)
     ).reshape(-1)
-    counts = lax.dynamic_slice_in_dim(slot_count, side * dst_rows, dst_rows, 0)
     counts = counts.astype(jnp.float32)[None, :]
+    ranks = ranks.astype(jnp.float32)[None, :]
     return attend(
-        slots, shared, counts, out_weight, far, nears, capacity, part, feat, heads, block
+        slots, levels, shared, counts, ranks, out_weight, far, nears,
+        capacity, part, feat, heads, block, step,
     )
 
 

time: 76.9 us -> 74.7 us (0.971)
  waiting for transfers between devices: 34.7 us -> 29.8 us
  local copies, waits for them, and re-layouts: 3 us -> 4.36 us
  starting transfers between devices: 17.3 us -> 18.2 us
  other arithmetic: 0.22 us -> 1.02 us
    ppermute x1, waiting for transfers between devices: 19.5 us -> 15.8 us  [local(): lax.ppermute(own, 'node', [(i, (i + half) % groups) for i in range(groups)])]
    unnamed x16, local copies, waits for them, and re-layouts: 0.8 us -> 2.07 us
    ppermute x2, waiting for transfers between devices: 10.4 us -> 9.21 us  [passed_round(): lax.ppermute(values, 'head', [(i, (i + step) % sides) for i in range(side...]
    ppermute x2, starting transfers between devices: 2.14 us -> 3.16 us  [passed_round(): lax.ppermute(values, 'head', [(i, (i + step) % sides) for i in range(side...]
  transfers between devices with their start and end apart: 6 -> 6, of which waited for: 4 -> 3; matrix products, arithmetic and copies ran while one was open for 2% -> 4% of each run, Pallas kernels for 6% -> 7%
where the time goes in v2:
time: 74.7 us; the launch traced here: 74 us
  waiting for transfers between devices  29.8 us (40%)
  Pallas kernels  20.2 us (27%)
  starting transfers between devices  18.2 us (24%)
  local copies, waits for them, and re-layouts  4.36 us (6%)
  other arithmetic  1.02 us (1%)
    ppermute x1, waiting for transfers between devices, local(): lax.ppermute(own, 'node', [(i, (i + half) % groups) for i in range(groups)])  15.8 us
    all_to_all x3, starting transfers between devices, within(): lax.all_to_all(values, 'node', split_axis=0, concat_axis=0, axis_index_gr...  12.4 us
    pallas_call x1, Pallas kernels, attend(): pl.pallas_call(functools.partial(attend_kernel, near_total=len(nears), wh...  11.5 us
    ppermute x2, waiting for transfers between devices, passed_round(): lax.ppermute(values, 'head', [(i, (i + step) % sides) for i in range(side...  9.21 us
    pallas_call x2, Pallas kernels, pick_rows(): pl.pallas_call(functools.partial(pick_kernel, stride=stride, part=part, p...  8.72 us
    all_to_all x3, waiting for transfers between devices, within(): lax.all_to_all(values, 'node', split_axis=0, concat_axis=0, axis_index_gr...  4.76 us
    ppermute x2, starting transfers between devices, passed_round(): lax.ppermute(values, 'head', [(i, (i + step) % sides) for i in range(side...  3.16 us
    ppermute x1, starting transfers between devices, local(): lax.ppermute(own, 'node', [(i, (i + half) % groups) for i in range(groups)])  2.66 us
  transfers between devices with their start and end apart: 6, of which 3 were waited for; matrix products, arithmetic and copies ran while one was open for 4% of the time, Pallas kernels for 7%

profile of v2, /device:TPU:0, one launch (start us, length us, event | category | flops | bytes accessed | tf_op | source)
XLA Modules:
  0.0 74.0 jit_solution(13566986153378667904)
XLA Ops:
  0.0 0.8 %copy-done.2 = s32[1,16,512]{2,1,0:T(8,128)S(1)} copy-done((s32[1,16,512]{2,1,0:T(8,128)S(1)}, s32[1,16,512]{2,1,0:T(8,128)}, u32[]{:S(2)}) %copy-start.2) | copy-done | bytes 32792
  0.8 0.2 rev.3
  1.0 0.6 reshape.67
  1.7 5.3 %all-to-all-start = ((s32[8,8,128]{2,1,0:T(8,128)}), s32[8,8,128]{2,1,0:T(8,128)S(1)}, u32[]{:S(2)}, u32[]{:S(2)}) async-start(s32[8,8,128]{2,1,0:T(8,128)} %reshape.67), calls=%async_computation | async-start | bytes 65536 | tf_op jit(solution)/shard_map/all_to_all | solution.py:389
  6.9 4.8 %all-to-all-done = s32[8,8,128]{2,1,0:T(8,128)S(1)} async-done(((s32[8,8,128]{2,1,0:T(8,128)}), s32[8,8,128]{2,1,0:T(8,128)S(1)}, u32[]{:S(2)}, u32[]{:S(2)}) %all-to-all-start) | async-done | bytes 32800 | tf_op jit(solution)/shard_map/all_to_all | solution.py:389
  11.7 3.9 %pick.3 = bf16[8,208,128]{2,1,0:T(8,128)(2,1)} custom-call(s32[1]{0:T(128)} %bitcast.10.begin, s32[8192]{0:T(1024)S(1)} %bitcast.19, bf16[100,2048]{1,0:T(8,128)(2,1)} %bitcast.22), custom_call_target="tpu_custom_call" | custom-call | tf_op jit(solution)/shard_map/pick/pallas_call | solution.py:88
  15.6 3.6 %all-to-all-start.2 = ((bf16[8,208,128]{2,1,0:T(8,128)(2,1)}), bf16[8,208,128]{2,1,0:T(8,128)(2,1)S(1)}, u32[]{:S(2)}, u32[]{:S(2)}) async-start(bf16[8,208,128]{2,1,0:T(8,128)(2,1)} %pick.3), calls=%async_computation.2 | async-start | bytes 851968 | tf_op jit(solution)/shard_map/all_to_all | solution.py:389
  19.3 2.7 %collective-permute-start.1 = (bf16[100,2048]{1,0:T(8,128)(2,1)S(1)}, bf16[100,2048]{1,0:T(8,128)(2,1)S(1)}, u32[]{:S(2)}, u32[]{:S(2)}) collective-permute-start(bf16[100,2048]{1,0:T(8,128)(2,1)S(1)} %bitcast.23), channel_id=1, source_target_pairs={{0,16},{2,18},{4,20},{6,22},{8,24},{10,26},{12,28},{14,30},{16,0},... | collective-permute-start | bytes 1228808 | tf_op jit(solution)/shard_map/ppermute | solution.py:386
  21.9 0.1 reshape.60
  22.2 0.6 copy-done.6
  23.1 1.6 %collective-permute-start = (bf16[106,256]{1,0:T(8,128)(2,1)S(1)}, bf16[106,256]{1,0:T(8,128)(2,1)S(1)}, u32[]{:S(2)}, u32[]{:S(2)}) collective-permute-start(bf16[106,256]{1,0:T(8,128)(2,1)S(1)} %concatenate.8), channel_id=1, source_target_pairs={{0,1},{1,0},{2,3},{3,2},{4,5},{5,4},{6,7},{7,6},{8,9},{9,8},{10,11... | collective-permute-start | bytes 162824 | tf_op jit(solution)/shard_map/ppermute | solution.py:351
  24.6 0.7 copy-done.7
  25.4 0.2 convert_reduce_fusion
  25.6 15.8 %collective-permute-done.1.features = bf16[100,2048]{1,0:T(8,128)(2,1)S(1)} collective-permute-done((bf16[100,2048]{1,0:T(8,128)(2,1)S(1)}, bf16[100,2048]{1,0:T(8,128)(2,1)S(1)}, u32[]{:S(2)}, u32[]{:S(2)}) %collective-permute-start.1) | collective-permute-done | bytes 409632 | tf_op jit(solution)/shard_map/ppermute | solution.py:386
  41.4 4.8 %pick.2 = bf16[8,416,128]{2,1,0:T(8,128)(2,1)} custom-call(s32[1]{0:T(128)} %constant.145.clone.1.begin, s32[8192]{0:T(1024)S(1)} %bitcast.20, bf16[100,2048]{1,0:T(8,128)(2,1)S(1)} %collective-permute-done.1.features), custom_call_target="tpu_custom_call" | custom-call | tf_op jit(solution)/shard_map/pick/pallas_call | solution.py:88
  46.3 3.6 %all-to-all-start.1 = ((bf16[8,416,128]{2,1,0:T(8,128)(2,1)}), bf16[8,416,128]{2,1,0:T(8,128)(2,1)S(1)}, u32[]{:S(2)}, u32[]{:S(2)}) async-start(bf16[8,416,128]{2,1,0:T(8,128)(2,1)} %pick.2), calls=%async_computation.1 | async-start | bytes 1703936 | tf_op jit(solution)/shard_map/all_to_all | solution.py:389
  49.9 0.1 fusion.19
  50.0 0.2 convolution_convert_fusion
  50.3 0.1 slice.3
  50.4 1.6 %collective-permute-start.2 = (bf16[8,208,128]{2,1,0:T(8,128)(2,1)S(1)}, bf16[8,208,128]{2,1,0:T(8,128)(2,1)S(1)}, u32[]{:S(2)}, u32[]{:S(2)}) collective-permute-start(bf16[8,208,128]{2,1,0:T(8,128)(2,1)S(1)} %all-to-all-done.2.refs_7_), channel_id=1, source_target_pairs={{0,1},{1,0},{2,3},{3,2},{4,5},{5,4},{6,7},{7,6},{8,9},{9,8},{10,11... | collective-permute-start | bytes 1277960 | tf_op jit(solution)/shard_map/ppermute | solution.py:351
  52.0 0.5 and_select_fusion.refs_1_
  52.6 0.7 reshape.59.refs_0_
  53.3 9.2 %collective-permute-done.2.refs_8_ = bf16[8,208,128]{2,1,0:T(8,128)(2,1)S(1)} collective-permute-done((bf16[8,208,128]{2,1,0:T(8,128)(2,1)S(1)}, bf16[8,208,128]{2,1,0:T(8,128)(2,1)S(1)}, u32[]{:S(2)}, u32[]{:S(2)}) %collective-permute-start.2) | collective-permute-done | bytes 426016 | tf_op jit(solution)/shard_map/ppermute | solution.py:351
  62.5 11.5 %attend.1 = bf16[256,512]{1,0:T(8,128)(2,1)} custom-call(s32[4096]{0:T(1024)} %reshape.59.refs_0_, s32[8]{0:T(128)} %and_select_fusion.refs_1_, bf16[2,106,256]{2,1,0:T(8,128)(2,1)S(1)} %pad_maximum_fusion.refs_2_, f32[1,256]{1,0:T(1,128)S(1)} %get-tuple-element.11.refs_3_, f32[1,256]{1,0:T(1,128)S(1)} %bitcast.21, bf16[512,512]{1,0:T(8,128)(2,1)S(1)} %copy-done, ...), custom_call_target="tpu_custom_call" | custom-call | tf_op jit(solution)/shard_map/attend/pallas_call | solution.py:284
  (36 shorter events, 0.8 us)
Async XLA Ops:
  0.0 0.8 %copy-start.2 = (s32[1,16,512]{2,1,0:T(8,128)S(1)}, s32[1,16,512]{2,1,0:T(8,128)}, u32[]{:S(2)}) copy-start(s32[1,16,512]{2,1,0:T(8,128)} %param.12) | copy-start | bytes 98308
  1.7 10.0 %all-to-all-start = ((s32[8,8,128]{2,1,0:T(8,128)}), s32[8,8,128]{2,1,0:T(8,128)S(1)}, u32[]{:S(2)}, u32[]{:S(2)}) async-start(s32[8,8,128]{2,1,0:T(8,128)} %reshape.67), calls=%async_computation | async-start | bytes 65536 | tf_op jit(solution)/shard_map/all_to_all | solution.py:389
  15.6 3.7 %copy-start.1 = (bf16[2048,100]{0,1:T(8,128)(2,1)S(1)}, bf16[2048,100]{0,1:T(8,128)(2,1)}, u32[]{:S(2)}) copy-start(bf16[2048,100]{0,1:T(8,128)(2,1)} %param.8) | copy-start | bytes 1228804
  15.6 6.3 %copy-start.5 = (f32[4,64]{1,0:T(4,128)S(1)}, f32[4,64]{1,0:T(4,128)}, u32[]{:S(2)}) copy-start(f32[4,64]{1,0:T(4,128)} %param.10) | copy-start | bytes 3076
  15.6 7.4 %copy-start.3 = (bf16[100,256]{1,0:T(8,128)(2,1)S(1)}, bf16[100,256]{1,0:T(8,128)(2,1)}, u32[]{:S(2)}) copy-start(bf16[100,256]{1,0:T(8,128)(2,1)} %param.9) | copy-start | bytes 153604
  15.6 30.7 %all-to-all-start.2 = ((bf16[8,208,128]{2,1,0:T(8,128)(2,1)}), bf16[8,208,128]{2,1,0:T(8,128)(2,1)S(1)}, u32[]{:S(2)}, u32[]{:S(2)}) async-start(bf16[8,208,128]{2,1,0:T(8,128)(2,1)} %pick.3), calls=%async_computation.2 | async-start | bytes 851968 | tf_op jit(solution)/shard_map/all_to_all | solution.py:389
  19.3 22.2 %collective-permute-start.1 = (bf16[100,2048]{1,0:T(8,128)(2,1)S(1)}, bf16[100,2048]{1,0:T(8,128)(2,1)S(1)}, u32[]{:S(2)}, u32[]{:S(2)}) collective-permute-start(bf16[100,2048]{1,0:T(8,128)(2,1)S(1)} %bitcast.23), channel_id=1, source_target_pairs={{0,16},{2,18},{4,20},{6,22},{8,24},{10,26},{12,28},{14,30},{16,0},... | collective-permute-start | bytes 1228808 | tf_op jit(solution)/shard_map/ppermute | solution.py:386
  22.1 0.7 copy-start.6
  23.1 30.2 %collective-permute-start = (bf16[106,256]{1,0:T(8,128)(2,1)S(1)}, bf16[106,256]{1,0:T(8,128)(2,1)S(1)}, u32[]{:S(2)}, u32[]{:S(2)}) collective-permute-start(bf16[106,256]{1,0:T(8,128)(2,1)S(1)} %concatenate.8), channel_id=1, source_target_pairs={{0,1},{1,0},{2,3},{3,2},{4,5},{5,4},{6,7},{7,6},{8,9},{9,8},{10,11... | collective-permute-start | bytes 162824 | tf_op jit(solution)/shard_map/ppermute | solution.py:351
  24.6 0.7 copy-start.7
  46.3 3.6 %copy-start.4 = (s32[512,16]{0,1:T(8,128)S(1)}, s32[512,16]{0,1:T(8,128)}, u32[]{:S(2)}) copy-start(s32[512,16]{0,1:T(8,128)} %param.13) | copy-start | bytes 98308
  46.3 16.2 %all-to-all-start.1 = ((bf16[8,416,128]{2,1,0:T(8,128)(2,1)}), bf16[8,416,128]{2,1,0:T(8,128)(2,1)S(1)}, u32[]{:S(2)}, u32[]{:S(2)}) async-start(bf16[8,416,128]{2,1,0:T(8,128)(2,1)} %pick.2), calls=%async_computation.1 | async-start | bytes 1703936 | tf_op jit(solution)/shard_map/all_to_all | solution.py:389
  50.0 12.5 %copy-start = (bf16[512,512]{1,0:T(8,128)(2,1)S(1)}, bf16[512,512]{1,0:T(8,128)(2,1)}, u32[]{:S(2)}) copy-start(bf16[512,512]{1,0:T(8,128)(2,1)} %refs_5_.1) | copy-start | bytes 1572868
  50.4 12.2 %collective-permute-start.2 = (bf16[8,208,128]{2,1,0:T(8,128)(2,1)S(1)}, bf16[8,208,128]{2,1,0:T(8,128)(2,1)S(1)}, u32[]{:S(2)}, u32[]{:S(2)}) collective-permute-start(bf16[8,208,128]{2,1,0:T(8,128)(2,1)S(1)} %all-to-all-done.2.refs_7_), channel_id=1, source_target_pairs={{0,1},{1,0},{2,3},{3,2},{4,5},{5,4},{6,7},{7,6},{8,9},{9,8},{10,11... | collective-permute-start | bytes 1277960 | tf_op jit(solution)/shard_map/ppermute | solution.py:351

commit v3 on v2

--- a/solution.py
+++ b/solution.py
@@ -182,7 +182,7 @@
 def attend_kernel(
     *refs, near_total, whole, part_whole, capacity, part, piece, feat, heads, block, slot_total, step
 ):
-    slots, levels, shared, counts, ranks, out_weight, far = refs[:7]
+    slots, ends, shared, counts, ranks, out_weight, far = refs[:7]
     nears = refs[7 : 7 + near_total]
     (
         out, table, rows_even, rows_odd, z_even, z_odd, sums_even, sums_odd, hidden,
@@ -242,24 +242,21 @@
     first_stage(0, count)
     fetch(2, 0).start()
 
-    @pl.loop(0, blocks // 2)
-    def _(pair):
-        for turn in range(2):
-            number = 2 * pair + turn
-            first = pl.multiple_of(number * block, 8)
-            level = levels[number]
-            fetch(number + 1, 1 - turn).wait()
-            for used in range(step, slot_total + 1, step):
-
-                @pl.when(level == used // step)
-                def _(turn=turn, used=used, first=first):
-                    copy_rows(lists[1 - turn], table, rows[1 - turn], block * used)
-                    first_stage(1 - turn, block * used)
-                    combine(
-                        z[turn], sums[turn], live, hidden, rows[1 - turn], first, heads, block, used
-                    )
-
-            fetch(number + 3, 1 - turn).start()
+    for used in range(slot_total, 0, -step):
+        above = 0 if used == slot_total else ends[used // step]
+
+        @pl.loop(above, ends[used // step - 1])
+        def _(pair, used=used):
+            for turn in range(2):
+                number = 2 * pair + turn
+                first = pl.multiple_of(number * block, 8)
+                fetch(number + 1, 1 - turn).wait()
+                copy_rows(lists[1 - turn], table, rows[1 - turn], block * used)
+                first_stage(1 - turn, block * used)
+                combine(
+                    z[turn], sums[turn], live, hidden, rows[1 - turn], first, heads, block, used
+                )
+                fetch(number + 3, 1 - turn).start()
 
     fetch(0, 0).wait()
     fetch(0, 1).wait()
@@ -272,7 +269,7 @@
 
 
 def attend(
-    slots, levels, shared, counts, ranks, out_weight, far, nears,
+    slots, ends, shared, counts, ranks, out_weight, far, nears,
     capacity, part, feat, heads, block, step
 ):
     whole, _, piece = spare_split(capacity, feat)
@@ -320,7 +317,7 @@
         out_shape=jax.ShapeDtypeStruct((dst_rows, out_weight.shape[1]), jnp.bfloat16),
         name="attend",
     )(
-        slots, levels, *[here(values) for values in (shared, counts, ranks, out_weight, far, *nears)]
+        slots, ends, *[here(values) for values in (shared, counts, ranks, out_weight, far, *nears)]
     )
 
 
@@ -416,14 +413,16 @@
     counts = lax.dynamic_slice_in_dim(slot_count, side * dst_rows, dst_rows, 0)
     slots, counts, ranks = by_count(slots, counts)
     step = slot_total // 4 if slot_total % 4 == 0 else slot_total
-    levels = (counts[::block] + step - 1) // step
+    levels = jnp.arange(0, slot_total, step, dtype=jnp.int32)
+    largest = counts[:: 2 * block]
+    ends = jnp.sum((largest[None, :] > levels[:, None]).astype(jnp.int32), axis=1)
     slots = jnp.transpose(
         slots.reshape(dst_rows // block, block, slot_total), (0, 2, 1)
     ).reshape(-1)
     counts = counts.astype(jnp.float32)[None, :]
     ranks = ranks.astype(jnp.float32)[None, :]
     return attend(
-        slots, levels, shared, counts, ranks, out_weight, far, nears,
+        slots, ends, shared, counts, ranks, out_weight, far, nears,
         capacity, part, feat, heads, block, step,
     )
 

time: 74.7 us -> 74.3 us (level)
  the two profiles are of different devices: /device:TPU:0 before, /device:TPU:10 now
where the time goes in v3:
time: 74.3 us; the launch traced here: 72.9 us
  waiting for transfers between devices  26.1 us (35%)
  starting transfers between devices  20.4 us (27%)
  Pallas kernels  20.4 us (27%)
  local copies, waits for them, and re-layouts  4.36 us (6%)
  other arithmetic  1.22 us (2%)
    ppermute x1, waiting for transfers between devices, local(): lax.ppermute(own, 'node', [(i, (i + half) % groups) for i in range(groups)])  14.9 us
    all_to_all x3, starting transfers between devices, within(): lax.all_to_all(values, 'node', split_axis=0, concat_axis=0, axis_index_gr...  14.7 us
    pallas_call x1, Pallas kernels, attend(): pl.pallas_call(functools.partial(attend_kernel, near_total=len(nears), wh...  11.7 us
    ppermute x2, waiting for transfers between devices, passed_round(): lax.ppermute(values, 'head', [(i, (i + step) % sides) for i in range(side...  8.74 us
    pallas_call x2, Pallas kernels, pick_rows(): pl.pallas_call(functools.partial(pick_kernel, stride=stride, part=part, p...  8.74 us
    ppermute x2, starting transfers between devices, passed_round(): lax.ppermute(values, 'head', [(i, (i + step) % sides) for i in range(side...  3.16 us
    ppermute x1, starting transfers between devices, local(): lax.ppermute(own, 'node', [(i, (i + half) % groups) for i in range(groups)])  2.59 us
    all_to_all x3, waiting for transfers between devices, within(): lax.all_to_all(values, 'node', split_axis=0, concat_axis=0, axis_index_gr...  2.49 us
  transfers between devices with their start and end apart: 6, of which 3 were waited for; matrix products, arithmetic and copies ran while one was open for 4% of the time, Pallas kernels for 7%

profile of v3, /device:TPU:10, one launch (start us, length us, event | category | flops | bytes accessed | tf_op | source)
XLA Modules:
  0.0 72.9 jit_solution(6548756711115010932)
XLA Ops:
  0.0 0.8 %copy-done.2 = s32[1,16,512]{2,1,0:T(8,128)S(1)} copy-done((s32[1,16,512]{2,1,0:T(8,128)S(1)}, s32[1,16,512]{2,1,0:T(8,128)}, u32[]{:S(2)}) %copy-start.2) | copy-done | bytes 32792
  0.8 0.2 rev.3
  1.0 0.6 reshape.72
  1.7 4.2 %all-to-all-start = ((s32[8,8,128]{2,1,0:T(8,128)}), s32[8,8,128]{2,1,0:T(8,128)S(1)}, u32[]{:S(2)}, u32[]{:S(2)}) async-start(s32[8,8,128]{2,1,0:T(8,128)} %reshape.72), calls=%async_computation | async-start | bytes 65536 | tf_op jit(solution)/shard_map/all_to_all | solution.py:386
  5.9 2.5 %all-to-all-done = s32[8,8,128]{2,1,0:T(8,128)S(1)} async-done(((s32[8,8,128]{2,1,0:T(8,128)}), s32[8,8,128]{2,1,0:T(8,128)S(1)}, u32[]{:S(2)}, u32[]{:S(2)}) %all-to-all-start) | async-done | bytes 32800 | tf_op jit(solution)/shard_map/all_to_all | solution.py:386
  8.4 3.9 %pick.3 = bf16[8,208,128]{2,1,0:T(8,128)(2,1)} custom-call(s32[1]{0:T(128)} %bitcast.10.begin, s32[8192]{0:T(1024)S(1)} %bitcast.19, bf16[100,2048]{1,0:T(8,128)(2,1)} %bitcast.22), custom_call_target="tpu_custom_call" | custom-call | tf_op jit(solution)/shard_map/pick/pallas_call | solution.py:88
  12.3 5.8 %all-to-all-start.2 = ((bf16[8,208,128]{2,1,0:T(8,128)(2,1)}), bf16[8,208,128]{2,1,0:T(8,128)(2,1)S(1)}, u32[]{:S(2)}, u32[]{:S(2)}) async-start(bf16[8,208,128]{2,1,0:T(8,128)(2,1)} %pick.3), calls=%async_computation.2 | async-start | bytes 851968 | tf_op jit(solution)/shard_map/all_to_all | solution.py:386
  18.1 2.6 %collective-permute-start.1 = (bf16[100,2048]{1,0:T(8,128)(2,1)S(1)}, bf16[100,2048]{1,0:T(8,128)(2,1)S(1)}, u32[]{:S(2)}, u32[]{:S(2)}) collective-permute-start(bf16[100,2048]{1,0:T(8,128)(2,1)S(1)} %bitcast.23), channel_id=1, source_target_pairs={{0,16},{2,18},{4,20},{6,22},{8,24},{10,26},{12,28},{14,30},{16,0},... | collective-permute-start | bytes 1228808 | tf_op jit(solution)/shard_map/ppermute | solution.py:383
  20.7 0.1 reshape.65
  20.8 0.1 reshape.66
  21.0 0.6 copy-done.6
  21.9 1.6 %collective-permute-start = (bf16[106,256]{1,0:T(8,128)(2,1)S(1)}, bf16[106,256]{1,0:T(8,128)(2,1)S(1)}, u32[]{:S(2)}, u32[]{:S(2)}) collective-permute-start(bf16[106,256]{1,0:T(8,128)(2,1)S(1)} %concatenate.8), channel_id=1, source_target_pairs={{0,1},{1,0},{2,3},{3,2},{4,5},{5,4},{6,7},{7,6},{8,9},{9,8},{10,11... | collective-permute-start | bytes 162824 | tf_op jit(solution)/shard_map/ppermute | solution.py:348
  23.5 0.7 copy-done.7
  24.2 0.2 convert_reduce_fusion
  24.4 14.9 %collective-permute-done.1.features = bf16[100,2048]{1,0:T(8,128)(2,1)S(1)} collective-permute-done((bf16[100,2048]{1,0:T(8,128)(2,1)S(1)}, bf16[100,2048]{1,0:T(8,128)(2,1)S(1)}, u32[]{:S(2)}, u32[]{:S(2)}) %collective-permute-start.1) | collective-permute-done | bytes 409632 | tf_op jit(solution)/shard_map/ppermute | solution.py:383
  39.2 4.8 %pick.2 = bf16[8,416,128]{2,1,0:T(8,128)(2,1)} custom-call(s32[1]{0:T(128)} %constant.132.clone.1.begin, s32[8192]{0:T(1024)S(1)} %bitcast.20, bf16[100,2048]{1,0:T(8,128)(2,1)S(1)} %collective-permute-done.1.features), custom_call_target="tpu_custom_call" | custom-call | tf_op jit(solution)/shard_map/pick/pallas_call | solution.py:88
  44.1 4.6 %all-to-all-start.1 = ((bf16[8,416,128]{2,1,0:T(8,128)(2,1)}), bf16[8,416,128]{2,1,0:T(8,128)(2,1)S(1)}, u32[]{:S(2)}, u32[]{:S(2)}) async-start(bf16[8,416,128]{2,1,0:T(8,128)(2,1)} %pick.2), calls=%async_computation.1 | async-start | bytes 1703936 | tf_op jit(solution)/shard_map/all_to_all | solution.py:386
  48.9 0.2 convolution_convert_fusion
  49.1 0.1 slice.3
  49.2 1.6 %collective-permute-start.2 = (bf16[8,208,128]{2,1,0:T(8,128)(2,1)S(1)}, bf16[8,208,128]{2,1,0:T(8,128)(2,1)S(1)}, u32[]{:S(2)}, u32[]{:S(2)}) collective-permute-start(bf16[8,208,128]{2,1,0:T(8,128)(2,1)S(1)} %all-to-all-done.2.refs_7_), channel_id=1, source_target_pairs={{0,1},{1,0},{2,3},{3,2},{4,5},{5,4},{6,7},{7,6},{8,9},{9,8},{10,11... | collective-permute-start | bytes 1277960 | tf_op jit(solution)/shard_map/ppermute | solution.py:348
  50.8 0.8 %convert_reduce_fusion.1.refs_1_ = s32[4]{0:T(128)} fusion(s32[4]{0:T(128)S(1)} %slice.3, s32[4]{0:T(128)S(1)} %iota_multiply_fusion), kind=kLoop, calls=%fused_computation.87 | loop fusion | flops 44 | bytes 48 | tf_op jit(solution)/shard_map/reduce_sum | solution.py:418
  51.7 0.7 reshape.64.refs_0_
  52.4 8.7 %collective-permute-done.2.refs_8_ = bf16[8,208,128]{2,1,0:T(8,128)(2,1)S(1)} collective-permute-done((bf16[8,208,128]{2,1,0:T(8,128)(2,1)S(1)}, bf16[8,208,128]{2,1,0:T(8,128)(2,1)S(1)}, u32[]{:S(2)}, u32[]{:S(2)}) %collective-permute-start.2) | collective-permute-done | bytes 426016 | tf_op jit(solution)/shard_map/ppermute | solution.py:348
  61.2 11.7 %attend.1 = bf16[256,512]{1,0:T(8,128)(2,1)} custom-call(s32[4096]{0:T(1024)} %reshape.64.refs_0_, s32[4]{0:T(128)} %convert_reduce_fusion.1.refs_1_, bf16[2,106,256]{2,1,0:T(8,128)(2,1)S(1)} %pad_maximum_fusion.refs_2_, f32[1,256]{1,0:T(1,128)S(1)} %get-tuple-element.11.refs_3_, f32[1,256]{1,0:T(1,128)S(1)} %bitcast.21, bf16[512,512]{1,0:T(8,128)(2,1)S(1)} %copy-done, ...), custom_call_target="tpu_custom_call" | custom-call | tf_op jit(solution)/shard_map/attend/pallas_call | solution.py:281
  (37 shorter events, 0.8 us)
Async XLA Ops:
  0.0 0.8 %copy-start.2 = (s32[1,16,512]{2,1,0:T(8,128)S(1)}, s32[1,16,512]{2,1,0:T(8,128)}, u32[]{:S(2)}) copy-start(s32[1,16,512]{2,1,0:T(8,128)} %param.12) | copy-start | bytes 98308
  1.7 6.7 %all-to-all-start = ((s32[8,8,128]{2,1,0:T(8,128)}), s32[8,8,128]{2,1,0:T(8,128)S(1)}, u32[]{:S(2)}, u32[]{:S(2)}) async-start(s32[8,8,128]{2,1,0:T(8,128)} %reshape.72), calls=%async_computation | async-start | bytes 65536 | tf_op jit(solution)/shard_map/all_to_all | solution.py:386
  12.3 5.9 %copy-start.1 = (bf16[2048,100]{0,1:T(8,128)(2,1)S(1)}, bf16[2048,100]{0,1:T(8,128)(2,1)}, u32[]{:S(2)}) copy-start(bf16[2048,100]{0,1:T(8,128)(2,1)} %param.8) | copy-start | bytes 1228804
  12.3 8.4 %copy-start.5 = (f32[4,64]{1,0:T(4,128)S(1)}, f32[4,64]{1,0:T(4,128)}, u32[]{:S(2)}) copy-start(f32[4,64]{1,0:T(4,128)} %param.10) | copy-start | bytes 3076
  12.3 9.5 %copy-start.3 = (bf16[100,256]{1,0:T(8,128)(2,1)S(1)}, bf16[100,256]{1,0:T(8,128)(2,1)}, u32[]{:S(2)}) copy-start(bf16[100,256]{1,0:T(8,128)(2,1)} %param.9) | copy-start | bytes 153604
  12.3 31.8 %all-to-all-start.2 = ((bf16[8,208,128]{2,1,0:T(8,128)(2,1)}), bf16[8,208,128]{2,1,0:T(8,128)(2,1)S(1)}, u32[]{:S(2)}, u32[]{:S(2)}) async-start(bf16[8,208,128]{2,1,0:T(8,128)(2,1)} %pick.3), calls=%async_computation.2 | async-start | bytes 851968 | tf_op jit(solution)/shard_map/all_to_all | solution.py:386
  18.1 21.1 %collective-permute-start.1 = (bf16[100,2048]{1,0:T(8,128)(2,1)S(1)}, bf16[100,2048]{1,0:T(8,128)(2,1)S(1)}, u32[]{:S(2)}, u32[]{:S(2)}) collective-permute-start(bf16[100,2048]{1,0:T(8,128)(2,1)S(1)} %bitcast.23), channel_id=1, source_target_pairs={{0,16},{2,18},{4,20},{6,22},{8,24},{10,26},{12,28},{14,30},{16,0},... | collective-permute-start | bytes 1228808 | tf_op jit(solution)/shard_map/ppermute | solution.py:383
  20.9 0.7 copy-start.6
  21.9 30.5 %collective-permute-start = (bf16[106,256]{1,0:T(8,128)(2,1)S(1)}, bf16[106,256]{1,0:T(8,128)(2,1)S(1)}, u32[]{:S(2)}, u32[]{:S(2)}) collective-permute-start(bf16[106,256]{1,0:T(8,128)(2,1)S(1)} %concatenate.8), channel_id=1, source_target_pairs={{0,1},{1,0},{2,3},{3,2},{4,5},{5,4},{6,7},{7,6},{8,9},{9,8},{10,11... | collective-permute-start | bytes 162824 | tf_op jit(solution)/shard_map/ppermute | solution.py:348
  23.4 0.7 copy-start.7
  44.1 4.7 %copy-start.4 = (s32[512,16]{0,1:T(8,128)S(1)}, s32[512,16]{0,1:T(8,128)}, u32[]{:S(2)}) copy-start(s32[512,16]{0,1:T(8,128)} %param.13) | copy-start | bytes 98308
  44.1 17.0 %all-to-all-start.1 = ((bf16[8,416,128]{2,1,0:T(8,128)(2,1)}), bf16[8,416,128]{2,1,0:T(8,128)(2,1)S(1)}, u32[]{:S(2)}, u32[]{:S(2)}) async-start(bf16[8,416,128]{2,1,0:T(8,128)(2,1)} %pick.2), calls=%async_computation.1 | async-start | bytes 1703936 | tf_op jit(solution)/shard_map/all_to_all | solution.py:386
  48.9 12.3 %copy-start = (bf16[512,512]{1,0:T(8,128)(2,1)S(1)}, bf16[512,512]{1,0:T(8,128)(2,1)}, u32[]{:S(2)}) copy-start(bf16[512,512]{1,0:T(8,128)(2,1)} %refs_5_.1) | copy-start | bytes 1572868
  49.2 11.9 %collective-permute-start.2 = (bf16[8,208,128]{2,1,0:T(8,128)(2,1)S(1)}, bf16[8,208,128]{2,1,0:T(8,128)(2,1)S(1)}, u32[]{:S(2)}, u32[]{:S(2)}) collective-permute-start(bf16[8,208,128]{2,1,0:T(8,128)(2,1)S(1)} %all-to-all-done.2.refs_7_), channel_id=1, source_target_pairs={{0,1},{1,0},{2,3},{3,2},{4,5},{5,4},{6,7},{7,6},{8,9},{9,8},{10,11... | collective-permute-start | bytes 1277960 | tf_op jit(solution)/shard_map/ppermute | solution.py:348
